TPU v7x, 32 devices: a whole 2x2x4 slice. The times are simulated.
32 devices in a mesh: tm: 4 (over y, x), paths: 8 (over z, core).
Axes of the slice: x: 2, y: 2, z: 4, core: 2. Of those that a mesh axis runs over, the one named last changes fastest.
Arguments:
- returns: bfloat16 [128, 4096, 256], P('tm', 'paths'), may hold values from -0.15917969 to 0.15917969
- weights: bfloat16 [256, 64], P('paths'), may hold values from -0.375 to 0.375
Outputs:
- drawdown: float32 [64, 4096], P('tm', 'paths')
All inputs are finite; a program needn't handle non-finite values.
Results may differ from a plain program's by a relative error of at most 0.0003.
Values may be sent and summed in bfloat16 or wider, within the bound.
A program may use at most 64 MiB of HBM per device.

v0:
```python
import functools

import jax
import jax.numpy as jnp
from jax import lax
from jax.experimental import pallas as pl
from jax.experimental.pallas import tpu as pltpu
from jax.sharding import PartitionSpec as P

MESH = pl.DeviceIdType.MESH
CHUNKS = 2
ROWS = 32


def kernel(
    n_tm, n_paths, ret_hbm, w_hbm, out_ref,
    ret, w_ref, wbuf, prof, send, recv, load_sem, own_sem, wsend_sem, wrecv_sem, send_sem, recv_sem,
):
    steps, paths, assets = ret.shape
    ports = w_ref.shape[1]
    block = ports // n_tm
    width = paths // CHUNKS
    half = width // 2
    groups = 1
    tm = lax.axis_index("tm")
    me = lax.axis_index("paths")

    def load(c, g):
        part = (pl.ds(g * steps, steps), pl.ds(c * width, width))
        return pltpu.make_async_copy(ret_hbm.at[part], ret.at[part], load_sem.at[c, g])

    own = pltpu.make_async_copy(w_hbm, w_ref, own_sem)
    own.start()
    for c in range(CHUNKS):
        for g in range(groups):
            load(c, g).start()

    barrier = pltpu.get_barrier_semaphore()
    for d in range(1, n_paths):
        pl.semaphore_signal(
            barrier, inc=1, device_id=(tm, lax.rem(me + d, n_paths)), device_id_type=MESH
        )
    for d in range(1, n_tm):
        pl.semaphore_signal(
            barrier, inc=1, device_id=(lax.rem(tm + d, n_tm), me), device_id_type=MESH
        )
    own.wait()
    pl.semaphore_wait(barrier, n_paths - 1 + n_tm - 1)

    def weight_copy(d):
        return pltpu.make_async_remote_copy(
            src_ref=w_ref,
            dst_ref=wbuf.at[me],
            send_sem=wsend_sem.at[d - 1],
            recv_sem=wrecv_sem.at[d - 1],
            device_id=(tm, lax.rem(me + d, n_paths)),
            device_id_type=MESH,
        )

    def weight_arrival(d):
        return pltpu.make_async_remote_copy(
            src_ref=w_ref,
            dst_ref=wbuf.at[lax.rem(me + n_paths - d, n_paths)],
            send_sem=wsend_sem.at[d - 1],
            recv_sem=wrecv_sem.at[d - 1],
            device_id=(tm, lax.rem(me + d, n_paths)),
            device_id_type=MESH,
        )

    for d in range(1, n_paths):
        weight_copy(d).start()
    wbuf[me] = w_ref[...]
    for d in range(1, n_paths):
        weight_arrival(d).wait_recv()

    held = wbuf[...].reshape(assets, ports)
    blank = jnp.zeros_like(held)
    both = jnp.concatenate(
        [jnp.concatenate([held, blank], axis=1), jnp.concatenate([blank, held], axis=1)], axis=0
    )

    def block_copy(c, d, slot):
        return pltpu.make_async_remote_copy(
            src_ref=send.at[c, lax.rem(tm + d, n_tm)],
            dst_ref=recv.at[c, slot],
            send_sem=send_sem.at[c, d - 1],
            recv_sem=recv_sem.at[c, d - 1],
            device_id=(lax.rem(tm + d, n_tm), me),
            device_id_type=MESH,
        )

    for c in range(CHUNKS):
        first = pl.ds(c * width, half)
        second = pl.ds(c * width + half, half)
        for g in range(groups):
            load(c, g).wait()
            when = pl.ds(g * steps, steps)
            left = ret[when, first, :].reshape(steps * half, assets)
            right = ret[when, second, :].reshape(steps * half, assets)
            prof[c, when] = jnp.dot(
                jnp.concatenate([left, right], axis=1), both, preferred_element_type=jnp.float32
            ).reshape(steps, half, 2 * ports)
        pieces = []
        for r in range(0, half, ROWS):
            value = prof[c, 0, pl.ds(r, ROWS)]
            high, low, fall = value, value, jnp.zeros_like(value)
            for t in range(1, steps):
                value = value + prof[c, t, pl.ds(r, ROWS)]
                high = jnp.maximum(high, value)
                low = jnp.minimum(low, value)
                fall = jnp.maximum(fall, high - value)
            pieces.append((value, high, fall, low))
        for k in range(4):
            whole = jnp.concatenate([piece[k] for piece in pieces], axis=0).T
            for b in range(n_tm):
                rows = b * block
                send[c, b, k, :, 0:half] = whole[rows : rows + block]
                send[c, b, k, :, half:width] = whole[ports + rows : ports + rows + block]
        for d in range(1, n_tm):
            block_copy(c, d, tm).start()
        recv[c, tm] = send[c, tm]

    for c in range(CHUNKS):
        for d in range(1, n_tm):
            block_copy(c, d, lax.rem(tm + n_tm - d, n_tm)).wait_recv()
        level = jnp.zeros((block, width), jnp.float32)
        peak, deepest = level, level
        for s in range(n_tm):
            deepest = jnp.maximum(deepest, recv[c, s, 2])
            deepest = jnp.maximum(deepest, peak - (level + recv[c, s, 3]))
            peak = jnp.maximum(peak, level + recv[c, s, 1])
            level = level + recv[c, s, 0]
        out_ref[:, pl.ds(c * width, width)] = deepest

    for d in range(1, n_paths):
        weight_copy(d).wait_send()
    for c in range(CHUNKS):
        for d in range(1, n_tm):
            block_copy(c, d, tm).wait_send()


def solution(mesh):
    n_tm, n_paths = mesh.shape["tm"], mesh.shape["paths"]

    def shards(returns, weights):
        steps, paths, assets = returns.shape
        share, ports = weights.shape
        block, width = ports // n_tm, paths // CHUNKS
        dma = pltpu.SemaphoreType.DMA
        return pl.pallas_call(
            functools.partial(kernel, n_tm, n_paths),
            out_shape=jax.ShapeDtypeStruct((block, paths), jnp.float32),
            in_specs=[
                pl.BlockSpec(memory_space=pltpu.HBM),
                pl.BlockSpec(memory_space=pltpu.HBM),
            ],
            out_specs=pl.BlockSpec(memory_space=pltpu.VMEM),
            scratch_shapes=[
                pltpu.VMEM((steps, paths, assets), returns.dtype),
                pltpu.VMEM((share, ports), weights.dtype),
                pltpu.VMEM((n_paths, share, ports), weights.dtype),
                pltpu.VMEM((CHUNKS, steps, width // 2, 2 * ports), jnp.float32),
                pltpu.VMEM((CHUNKS, n_tm, 4, block, width), jnp.float32),
                pltpu.VMEM((CHUNKS, n_tm, 4, block, width), jnp.float32),
                dma((CHUNKS, 1)),
                dma,
                dma((n_paths - 1,)),
                dma((n_paths - 1,)),
                dma((CHUNKS, n_tm - 1)),
                dma((CHUNKS, n_tm - 1)),
            ],
            compiler_params=pltpu.CompilerParams(
                collective_id=0, has_side_effects=True, vmem_limit_bytes=63 << 20
            ),
        )(returns, weights)

    in_specs = (P("tm", "paths", None), P("paths", None))
    out_specs = P("tm", "paths")
    return jax.shard_map(shards, mesh=mesh, in_specs=in_specs, out_specs=out_specs, check_vma=False)
```

profile of v0, /device:TPU:0, one launch (start us, length us, event | category | flops | bytes accessed | tf_op | source)
XLA Modules:
  0.0 21.6 jit_solution(2489891606481771376)
XLA Ops:
  0.0 20.2 %shard_map.28 = f32[16,512]{1,0:T(8,128)} custom-call(bf16[32,512,256]{2,1,0:T(8,128)(2,1)} %ret_hbm.1, bf16[32,64]{1,0:T(8,128)(2,1)} %w_hbm.1), custom_call_target="tpu_custom_call" | custom-call | tf_op jit(solution)/shard_map/pallas_call | solution.py:150
  20.2 1.4 %copy.4 = f32[16,512]{1,0:T(8,128)} copy(f32[16,512]{1,0:T(8,128)} %shard_map.28) | data formatting | bytes 65536
where the time goes:
time: 21.7 us; the launch traced here: 21.6 us
  Pallas kernels  20.2 us (93%)
  local copies, waits for them, and re-layouts  1.38 us (6%)
    pallas_call x1, Pallas kernels, shards(): pl.pallas_call(functools.partial(kernel, n_tm, n_paths), out_shape=jax.Sh...  20.2 us
    unnamed x1, local copies, waits for them, and re-layouts  1.38 us

commit v1 on v0

--- a/solution.py
+++ b/solution.py
@@ -170,9 +170,12 @@
                 dma((CHUNKS, n_tm - 1)),
             ],
             compiler_params=pltpu.CompilerParams(
-                collective_id=0, has_side_effects=True, vmem_limit_bytes=63 << 20
+                collective_id=0, has_side_effects=True, vmem_limit_bytes=32 << 20
             ),
-        )(returns, weights)
+        )(
+            pltpu.with_memory_space_constraint(returns, pltpu.HBM),
+            pltpu.with_memory_space_constraint(weights, pltpu.HBM),
+        )
 
     in_specs = (P("tm", "paths", None), P("paths", None))
     out_specs = P("tm", "paths")

time: 21.7 us -> 20.4 us (0.940)
  local copies, waits for them, and re-layouts: 1.38 us -> 0.62 us
  Pallas kernels: 20.2 us -> 19.6 us
    unnamed x1, local copies, waits for them, and re-layouts: 1.38 us -> 0.62 us
    pallas_call x1, Pallas kernels: 20.2 us -> 19.6 us  [shards(): pl.pallas_call(functools.partial(kernel, n_tm, n_paths), out_shape=jax.Sh...]
where the time goes in v1:
time: 20.4 us; the launch traced here: 20.2 us
  Pallas kernels  19.6 us (96%)
  local copies, waits for them, and re-layouts  0.62 us (3%)
    pallas_call x1, Pallas kernels, shards(): pl.pallas_call(functools.partial(kernel, n_tm, n_paths), out_shape=jax.Sh...  19.6 us
    unnamed x1, local copies, waits for them, and re-layouts  0.62 us

profile of v1, /device:TPU:0, one launch (start us, length us, event | category | flops | bytes accessed | tf_op | source)
XLA Modules:
  0.0 20.2 jit_solution(2586004941120287843)
XLA Ops:
  0.0 19.6 %shard_map.28 = f32[16,512]{1,0:T(8,128)S(1)} custom-call(bf16[32,512,256]{2,1,0:T(8,128)(2,1)} %ret_hbm.1, bf16[32,64]{1,0:T(8,128)(2,1)} %w_hbm.1), custom_call_target="tpu_custom_call" | custom-call | tf_op jit(solution)/shard_map/pallas_call | solution.py:150
  19.6 0.6 %copy.4 = f32[16,512]{1,0:T(8,128)} copy(f32[16,512]{1,0:T(8,128)S(1)} %shard_map.28) | data formatting | bytes 65536

commit v2 on v1

v2 whole, which is shorter than its diff:
```python
import functools

import jax
import jax.numpy as jnp
from jax import lax
from jax.experimental import pallas as pl
from jax.experimental.pallas import tpu as pltpu
from jax.sharding import PartitionSpec as P

MESH = pl.DeviceIdType.MESH
CHUNKS = 2
ROWS = 32
LOUD = 64
END, FALL, DIP, LOSS = range(4)
TOP = 2.0**15.75
TINY = 1e-30


def kernel(
    n_tm, n_paths, ret_hbm, w_hbm, out_ref,
    ret, own_w, pair_w, wbuf, part, more, send, recv, loud, louds,
    load_sem, own_sem, wsend_sem, wrecv_sem, send_sem, recv_sem, lsend_sem, lrecv_sem,
):
    steps, paths, assets = ret.shape
    ports = own_w.shape[1]
    block = ports // n_tm
    width = paths // CHUNKS
    half = width // 2
    depth = assets // 2
    subs = half // ROWS
    tm = lax.axis_index("tm")
    me = lax.axis_index("paths")
    near = (2 * me) // n_paths

    barrier = pltpu.get_barrier_semaphore()
    for d in range(1, n_paths):
        pl.semaphore_signal(
            barrier, inc=1, device_id=(tm, lax.rem(me + d, n_paths)), device_id_type=MESH
        )
    for d in range(1, n_tm):
        pl.semaphore_signal(
            barrier, inc=1, device_id=(lax.rem(tm + d, n_tm), me), device_id_type=MESH
        )

    own = pltpu.make_async_copy(w_hbm, own_w, own_sem)
    own.start()

    def load(c):
        rows = pl.ds(c * width, width)
        return pltpu.make_async_copy(ret_hbm.at[:, rows], ret.at[:, rows], load_sem.at[c])

    for c in range(CHUNKS):
        load(c).start()

    own.wait()
    pair_w[...] = jnp.concatenate([own_w[...], own_w[...]], axis=1)
    wbuf[me] = pair_w[...]
    pl.semaphore_wait(barrier, n_paths - 1 + n_tm - 1)

    def weight_copy(d, slot):
        return pltpu.make_async_remote_copy(
            src_ref=pair_w,
            dst_ref=wbuf.at[slot],
            send_sem=wsend_sem.at[d - 1],
            recv_sem=wrecv_sem.at[slot],
            device_id=(tm, lax.rem(me + d, n_paths)),
            device_id_type=MESH,
        )

    for d in range(1, n_paths):
        weight_copy(d, me).start()

    def loud_copy(d, slot):
        return pltpu.make_async_remote_copy(
            src_ref=loud,
            dst_ref=louds.at[slot],
            send_sem=lsend_sem.at[d - 1],
            recv_sem=lrecv_sem.at[d - 1],
            device_id=(lax.rem(tm + d, n_tm), me),
            device_id_type=MESH,
        )

    top = jnp.zeros((LOUD, assets), ret.dtype)
    for c in range(CHUNKS):
        load(c).wait()

        def scan_rows(t, top):
            for r in range(0, width, LOUD):
                top = jnp.maximum(top, jnp.abs(ret[t, pl.ds(c * width + r, LOUD)]))
            return top

        top = lax.fori_loop(0, steps, scan_rows, top)
    loud[...] = jnp.full(loud.shape, jnp.max(top.astype(jnp.float32)), jnp.float32)
    louds[tm] = loud[...]
    for d in range(1, n_tm):
        loud_copy(d, tm).start()

    def side(h):
        held = wbuf[pl.ds(h * (n_paths // 2), n_paths // 2)].reshape(depth, 2 * ports)
        left = lax.broadcasted_iota(jnp.int32, held.shape, 1) < ports
        blank = jnp.zeros_like(held)
        return jnp.concatenate([jnp.where(left, held, blank), jnp.where(left, blank, held)], axis=0)

    def product(c, i, h, both):
        cols = pl.ds(pl.multiple_of(h * depth, depth), depth)
        first = ret[:, pl.ds(c * width + i * ROWS, ROWS), cols].reshape(steps * ROWS, depth)
        second = ret[:, pl.ds(c * width + half + i * ROWS, ROWS), cols].reshape(steps * ROWS, depth)
        return jnp.dot(
            jnp.concatenate([first, second], axis=1), both, preferred_element_type=jnp.float32
        ).reshape(steps, ROWS, 2 * ports)

    def block_copy(c, d, slot):
        return pltpu.make_async_remote_copy(
            src_ref=send.at[c, lax.rem(tm + d, n_tm)],
            dst_ref=recv.at[c, slot],
            send_sem=send_sem.at[c, d - 1],
            recv_sem=recv_sem.at[c, d - 1],
            device_id=(lax.rem(tm + d, n_tm), me),
            device_id_type=MESH,
        )

    group = n_paths // 2
    for k in range(1, group):
        weight_copy(1, near * group + lax.rem(me + k, group)).wait_recv()
    both = side(near)
    for c in range(CHUNKS):
        for i in range(subs):
            part[c, i] = product(c, i, near, both)

    for k in range(group):
        weight_copy(1, (1 - near) * group + k).wait_recv()
    both = side(1 - near)
    for c in range(CHUNKS):
        for i in range(subs):
            more[c, i] = product(c, i, 1 - near, both)
        if c == 0:
            heavy = jnp.max(jnp.abs(wbuf[...].astype(jnp.float32)))
            scale = TOP / jnp.maximum(loud[0:1] * (heavy * (assets * steps)), TINY)
        pieces = []
        for i in range(subs):
            zero = jnp.zeros((ROWS, 2 * ports), jnp.float32)
            end, fall, dip, loss = zero, zero, zero, zero
            for t in range(steps):
                gain = part[c, i, t] + more[c, i, t]
                end = jnp.maximum(end - gain, 0.0)
                fall = jnp.maximum(fall, end)
                loss = loss - gain
                dip = jnp.maximum(dip, loss)
            figures = []
            for k, figure in enumerate((end, fall, dip, loss)):
                code = figure * scale
                code = code * code
                code = code * code
                code = code * code
                if k == LOSS:
                    code = jnp.where(figure < 0, -code, code)
                figures.append(code.astype(jnp.bfloat16))
            pieces.append(figures)
        for k in range(4):
            whole = jnp.concatenate([piece[k] for piece in pieces], axis=0).T
            for b in range(n_tm):
                rows = b * block
                send[c, b, k, :, 0:half] = whole[rows : rows + block]
                send[c, b, k, :, half:width] = whole[ports + rows : ports + rows + block]
        for d in range(1, n_tm):
            block_copy(c, d, tm).start()
        recv[c, tm] = send[c, tm]

    for d in range(1, n_tm):
        loud_copy(d, lax.rem(tm + n_tm - d, n_tm)).wait_recv()
    back = jnp.maximum(louds[:, 0:1] * (heavy * (assets * steps)), TINY) / TOP

    def figure(c, s, k):
        code = recv[c, s, k].astype(jnp.float32)
        size = jnp.exp(jnp.log(jnp.abs(code)) * 0.125) * jnp.tile(back[s], (1, width // back.shape[2]))
        return jnp.where(code < 0, -size, size) if k == LOSS else size

    for c in range(CHUNKS):
        for d in range(1, n_tm):
            block_copy(c, d, lax.rem(tm + n_tm - d, n_tm)).wait_recv()
        end, fall = figure(c, 0, END), figure(c, 0, FALL)
        for s in range(1, n_tm):
            fall = jnp.maximum(jnp.maximum(fall, figure(c, s, FALL)), end + figure(c, s, DIP))
            if s < n_tm - 1:
                end = jnp.maximum(end + figure(c, s, LOSS), figure(c, s, END))
        out_ref[:, pl.ds(c * width, width)] = fall

    for d in range(1, n_paths):
        weight_copy(d, me).wait_send()
    for d in range(1, n_tm):
        loud_copy(d, tm).wait_send()
        for c in range(CHUNKS):
            block_copy(c, d, tm).wait_send()


def solution(mesh):
    n_tm, n_paths = mesh.shape["tm"], mesh.shape["paths"]

    def shards(returns, weights):
        steps, paths, assets = returns.shape
        share, ports = weights.shape
        block, width = ports // n_tm, paths // CHUNKS
        subs = width // 2 // ROWS
        dma = pltpu.SemaphoreType.DMA
        return pl.pallas_call(
            functools.partial(kernel, n_tm, n_paths),
            out_shape=jax.ShapeDtypeStruct((block, paths), jnp.float32),
            in_specs=[
                pl.BlockSpec(memory_space=pltpu.HBM),
                pl.BlockSpec(memory_space=pltpu.HBM),
            ],
            out_specs=pl.BlockSpec(memory_space=pltpu.VMEM),
            scratch_shapes=[
                pltpu.VMEM((steps, paths, assets), returns.dtype),
                pltpu.VMEM((share, ports), weights.dtype),
                pltpu.VMEM((share, 2 * ports), weights.dtype),
                pltpu.VMEM((n_paths, share, 2 * ports), weights.dtype),
                pltpu.VMEM((CHUNKS, subs, steps, ROWS, 2 * ports), jnp.float32),
                pltpu.VMEM((CHUNKS, subs, steps, ROWS, 2 * ports), jnp.float32),
                pltpu.VMEM((CHUNKS, n_tm, 4, block, width), jnp.bfloat16),
                pltpu.VMEM((CHUNKS, n_tm, 4, block, width), jnp.bfloat16),
                pltpu.VMEM((8, 2 * ports), jnp.float32),
                pltpu.VMEM((n_tm, 8, 2 * ports), jnp.float32),
                dma((CHUNKS,)),
                dma,
                dma((n_paths - 1,)),
                dma((n_paths,)),
                dma((CHUNKS, n_tm - 1)),
                dma((CHUNKS, n_tm - 1)),
                dma((n_tm - 1,)),
                dma((n_tm - 1,)),
            ],
            compiler_params=pltpu.CompilerParams(
                collective_id=0, has_side_effects=True, vmem_limit_bytes=32 << 20
            ),
        )(
            pltpu.with_memory_space_constraint(returns, pltpu.HBM),
            pltpu.with_memory_space_constraint(weights, pltpu.HBM),
        )

    in_specs = (P("tm", "paths", None), P("paths", None))
    out_specs = P("tm", "paths")
    return jax.shard_map(shards, mesh=mesh, in_specs=in_specs, out_specs=out_specs, check_vma=False)
```

time: 20.4 us -> 16.6 us (0.81)
  Pallas kernels: 19.6 us -> 15.9 us
    pallas_call x1, Pallas kernels: 19.6 us -> 15.9 us  [shards(): pl.pallas_call(functools.partial(kernel, n_tm, n_paths), out_shape=jax.Sh...]
where the time goes in v2:
time: 16.6 us; the launch traced here: 16.5 us
  Pallas kernels  15.9 us (96%)
  local copies, waits for them, and re-layouts  0.62 us (4%)
    pallas_call x1, Pallas kernels, shards(): pl.pallas_call(functools.partial(kernel, n_tm, n_paths), out_shape=jax.Sh...  15.9 us
    unnamed x1, local copies, waits for them, and re-layouts  0.62 us

profile of v2, /device:TPU:0, one launch (start us, length us, event | category | flops | bytes accessed | tf_op | source)
XLA Modules:
  0.0 16.5 jit_solution(12541446095147701114)
XLA Ops:
  0.0 15.9 %shard_map.28 = f32[16,512]{1,0:T(8,128)S(1)} custom-call(bf16[32,512,256]{2,1,0:T(8,128)(2,1)} %ret_hbm.1, bf16[32,64]{1,0:T(8,128)(2,1)} %w_hbm.1), custom_call_target="tpu_custom_call" | custom-call | tf_op jit(solution)/shard_map/pallas_call | solution.py:205
  15.9 0.6 %copy.4 = f32[16,512]{1,0:T(8,128)} copy(f32[16,512]{1,0:T(8,128)S(1)} %shard_map.28) | data formatting | bytes 65536

commit v3 on v2

v3 whole, which is shorter than its diff:
```python
import functools

import jax
import jax.numpy as jnp
from jax import lax
from jax.experimental import pallas as pl
from jax.experimental.pallas import tpu as pltpu
from jax.sharding import PartitionSpec as P

MESH = pl.DeviceIdType.MESH
CHUNKS = 2
ROWS = 32
LOUD = 32
END, FALL, DIP, LOSS = range(4)
TOP = 2.0**15.75
TINY = 1e-30


def kernel(
    n_tm, n_paths, ret_hbm, w_hbm, out_ref,
    ret, own_w, pair_w, wbuf, part, more, send, recv, loud, louds,
    load_sem, own_sem, ready, near_sem, far_sem, wrecv_sem, send_sem, recv_sem, lsend_sem, lrecv_sem,
):
    steps, paths, assets = ret.shape
    ports = own_w.shape[1]
    block = ports // n_tm
    width = paths // CHUNKS
    half = width // 2
    depth = assets // 2
    subs = half // ROWS
    tm = lax.axis_index("tm")
    me = lax.axis_index("paths")
    share = own_w.shape[0]

    bits = [1 << i for i in range(n_tm.bit_length() - 1)]
    others = range(n_tm - 1, 0, -1)

    def across(k):
        other = tm
        for bit in (b for b in bits if b & k):
            other = other + bit - 2 * bit * ((tm // bit) % 2)
        return other

    half_axis = n_paths // 2
    upper = me // half_axis
    gate = half_axis - 1
    barrier = pltpu.get_barrier_semaphore()

    def greet(t, p):
        pl.semaphore_signal(barrier, inc=1, device_id=(t, p), device_id_type=MESH)

    def fellow(k):
        return upper * half_axis + (me + k) % half_axis

    def greet_upper():
        for p in range(half_axis, n_paths):
            greet(tm, p)

    pl.when(upper == 1)(lambda: greet(tm, gate))
    pl.when(upper == 0)(greet_upper)
    for k in range(1, half_axis):
        greet(tm, fellow(k))
    for k in bits:
        greet(across(k), me)

    own = pltpu.make_async_copy(w_hbm, own_w, own_sem)
    own.start()

    def load(c):
        rows = pl.ds(c * width, width)
        return pltpu.make_async_copy(ret_hbm.at[:, rows], ret.at[:, rows], load_sem.at[c])

    for c in range(CHUNKS):
        load(c).start(priority=1)

    own.wait()
    pair_w[...] = jnp.concatenate([own_w[0 : share // 2], own_w[share // 2 :]], axis=1)
    wbuf[me] = pair_w[...]
    crossing = jnp.logical_or(upper == 1, me == gate).astype(jnp.int32)
    pl.semaphore_wait(barrier, half_axis - 1 + len(bits) + half_axis * crossing)

    for k in (k for k in range(n_tm) if k.bit_count() == 2):
        pl.semaphore_signal(ready.at[k], inc=1, device_id=(across(k & -k), me), device_id_type=MESH)

    def block_of_weights(slot, count, target, sem):
        rows = pl.ds(slot, count)
        return pltpu.make_async_remote_copy(
            src_ref=wbuf.at[rows],
            dst_ref=wbuf.at[rows],
            send_sem=sem,
            recv_sem=wrecv_sem.at[slot],
            device_id=(tm, target),
            device_id_type=MESH,
        )

    def own_weights(target, sem):
        return pltpu.make_async_remote_copy(
            src_ref=pair_w,
            dst_ref=wbuf.at[me],
            send_sem=sem,
            recv_sem=wrecv_sem.at[me],
            device_id=(tm, target),
            device_id_type=MESH,
        )

    def arrival(slot, count):
        block_of_weights(slot, count, me, near_sem.at[0]).wait_recv()

    def send_down(act):
        def down():
            for p in range(half_axis):
                act(own_weights(p, far_sem.at[p]))

        pl.when(upper == 1)(down)

    def send_near(act):
        for k in range(half_axis - 1, 0, -1):
            act(own_weights(fellow(k), near_sem.at[k - 1]))

    def send_over(act):
        def over():
            for p in range(n_paths - 1, half_axis - 1, -1):
                act(block_of_weights(0, half_axis, p, far_sem.at[p - half_axis]))

        pl.when(me == gate)(over)

    def far_arrival():
        def shards():
            for p in range(half_axis, n_paths):
                arrival(p, 1)

        pl.when(upper == 1)(lambda: arrival(0, half_axis))
        pl.when(upper == 0)(shards)

    send_down(lambda copy: copy.start())
    send_near(lambda copy: copy.start())
    for k in range(1, half_axis):
        arrival(fellow(k), 1)
    send_over(lambda copy: copy.start())

    for p in range(2, len(bits) + 1):
        for k in (k for k in range(n_tm) if k.bit_count() == p):
            pl.semaphore_wait(ready.at[k], 1)
        for k in (k for k in range(n_tm) if k.bit_count() == p + 1):
            pl.semaphore_signal(ready.at[k], inc=1, device_id=(across(k & -k), me), device_id_type=MESH)

    def loud_copy(c, k, slot):
        return pltpu.make_async_remote_copy(
            src_ref=loud.at[c],
            dst_ref=louds.at[c, slot],
            send_sem=lsend_sem.at[c, k - 1],
            recv_sem=lrecv_sem.at[c, k - 1],
            device_id=(across(k), me),
            device_id_type=MESH,
        )

    def side(h):
        held = wbuf[pl.ds(h * half_axis, half_axis)]
        swap = jnp.concatenate([held[:, :, ports:], held[:, :, :ports]], axis=2)
        rows = jnp.concatenate([held[:, None], swap[:, None]], axis=1).reshape(depth, 2 * ports)
        spare = jnp.concatenate([swap[:, None], held[:, None]], axis=1).reshape(depth, 2 * ports)
        left = lax.broadcasted_iota(jnp.int32, rows.shape, 1) < ports
        blank = jnp.zeros_like(rows)
        return jnp.concatenate([jnp.where(left, rows, blank), jnp.where(left, blank, spare)], axis=0)

    def product(c, i, h, both):
        cols = pl.ds(pl.multiple_of(h * depth, depth), depth)
        first = ret[:, pl.ds(c * width + i * ROWS, ROWS), cols].reshape(steps * ROWS, depth)
        second = ret[:, pl.ds(c * width + half + i * ROWS, ROWS), cols].reshape(steps * ROWS, depth)
        return jnp.dot(
            jnp.concatenate([first, second], axis=1), both, preferred_element_type=jnp.float32
        ).reshape(steps, ROWS, 2 * ports)

    def block_copy(c, k, slot, first, count):
        figures = pl.ds(first, count)
        return pltpu.make_async_remote_copy(
            src_ref=send.at[c, across(k), figures],
            dst_ref=recv.at[c, slot, figures],
            send_sem=send_sem.at[c, k - 1],
            recv_sem=recv_sem.at[c, k - 1],
            device_id=(across(k), me),
            device_id_type=MESH,
        )

    def by_segment(s, act):
        pl.when(s == 0)(lambda: act(END, 2))
        pl.when(s == n_tm - 1)(lambda: act(FALL, 2))
        pl.when(jnp.logical_and(s > 0, s < n_tm - 1))(lambda: act(END, 4))

    def send_blocks(c, act):
        def blocks(first, count):
            for k in others:
                act(block_copy(c, k, tm, first, count))

        by_segment(tm, blocks)

    def block_arrival(c, k):
        s = across(k)
        by_segment(s, lambda first, count: block_copy(c, k, s, first, count).wait_recv())

    both = side(upper)
    for c in range(CHUNKS):
        load(c).wait()
        for i in range(subs):
            part[c, i] = product(c, i, upper, both)
        top = jnp.zeros((LOUD, assets), ret.dtype)
        for t in range(steps):
            for r in range(c * width, (c + 1) * width, LOUD):
                top = jnp.maximum(top, jnp.abs(ret[t, r : r + LOUD]))
        loud[c] = jnp.full(loud.shape[1:], jnp.max(top.astype(jnp.float32)), jnp.float32)
        for k in others:
            loud_copy(c, k, tm).start()
        louds[c, tm] = loud[c]

    far_arrival()
    both = side(1 - upper)
    for c in range(CHUNKS):
        for i in range(subs):
            more[c, i] = product(c, i, 1 - upper, both)
        if c == 0:
            heavy = jnp.max(jnp.abs(wbuf[...].astype(jnp.float32))) * (assets * steps)
        scale = TOP / jnp.maximum(loud[c, 0:1] * heavy, TINY)
        pieces = []
        for i in range(subs):
            zero = jnp.zeros((ROWS, 2 * ports), jnp.float32)
            end, fall, dip, loss = zero, zero, zero, zero
            for t in range(steps):
                gain = part[c, i, t] + more[c, i, t]
                end = jnp.maximum(end - gain, 0.0)
                fall = jnp.maximum(fall, end)
                loss = loss - gain
                dip = jnp.maximum(dip, loss)
            figures = []
            for k, figure in enumerate((end, fall, dip, loss)):
                code = figure * scale
                code = code * code
                code = code * code
                code = code * code
                if k == LOSS:
                    code = jnp.where(figure < 0, -code, code)
                figures.append(code.astype(jnp.bfloat16))
            pieces.append(figures)
        for k in range(4):
            whole = jnp.concatenate([piece[k] for piece in pieces], axis=0).T
            for b in range(n_tm):
                rows = b * block
                send[c, b, k, :, 0:half] = whole[rows : rows + block]
                send[c, b, k, :, half:width] = whole[ports + rows : ports + rows + block]
        send_blocks(c, lambda copy: copy.start())
        recv[c, tm] = send[c, tm]

    def figure(c, s, k, back):
        code = recv[c, s, k].astype(jnp.float32)
        size = jnp.exp(jnp.log(jnp.abs(code)) * 0.125) * back[s]
        return jnp.where(code < 0, -size, size) if k == LOSS else size

    for c in range(CHUNKS):
        for k in others:
            block_arrival(c, k)
            loud_copy(c, k, across(k)).wait_recv()
        back = jnp.maximum(louds[c, :, 0:1] * heavy, TINY) / TOP
        back = jnp.concatenate([back] * (width // back.shape[2]), axis=2)
        end, fall = figure(c, 0, END, back), figure(c, 0, FALL, back)
        for s in range(1, n_tm):
            fall = jnp.maximum(jnp.maximum(fall, figure(c, s, FALL, back)), end + figure(c, s, DIP, back))
            if s < n_tm - 1:
                end = jnp.maximum(end + figure(c, s, LOSS, back), figure(c, s, END, back))
        out_ref[:, pl.ds(c * width, width)] = fall

    send_down(lambda copy: copy.wait_send())
    send_near(lambda copy: copy.wait_send())
    send_over(lambda copy: copy.wait_send())
    for c in range(CHUNKS):
        for k in others:
            loud_copy(c, k, tm).wait_send()
        send_blocks(c, lambda copy: copy.wait_send())


def solution(mesh):
    n_tm, n_paths = mesh.shape["tm"], mesh.shape["paths"]

    def shards(returns, weights):
        steps, paths, assets = returns.shape
        share, ports = weights.shape
        block, width = ports // n_tm, paths // CHUNKS
        subs = width // 2 // ROWS
        dma = pltpu.SemaphoreType.DMA
        return pl.pallas_call(
            functools.partial(kernel, n_tm, n_paths),
            out_shape=jax.ShapeDtypeStruct((block, paths), jnp.float32),
            in_specs=[
                pl.BlockSpec(memory_space=pltpu.HBM),
                pl.BlockSpec(memory_space=pltpu.HBM),
            ],
            out_specs=pl.BlockSpec(memory_space=pltpu.VMEM),
            scratch_shapes=[
                pltpu.VMEM((steps, paths, assets), returns.dtype),
                pltpu.VMEM((share, ports), weights.dtype),
                pltpu.VMEM((share // 2, 2 * ports), weights.dtype),
                pltpu.VMEM((n_paths, share // 2, 2 * ports), weights.dtype),
                pltpu.VMEM((CHUNKS, subs, steps, ROWS, 2 * ports), jnp.float32),
                pltpu.VMEM((CHUNKS, subs, steps, ROWS, 2 * ports), jnp.float32),
                pltpu.VMEM((CHUNKS, n_tm, 4, block, width), jnp.bfloat16),
                pltpu.VMEM((CHUNKS, n_tm, 4, block, width), jnp.bfloat16),
                pltpu.VMEM((CHUNKS, 8, 2 * ports), jnp.float32),
                pltpu.VMEM((CHUNKS, n_tm, 8, 2 * ports), jnp.float32),
                dma((CHUNKS,)),
                dma,
                pltpu.SemaphoreType.REGULAR((n_tm,)),
                dma((n_paths // 2 - 1,)),
                dma((n_paths // 2,)),
                dma((n_paths,)),
                dma((CHUNKS, n_tm - 1)),
                dma((CHUNKS, n_tm - 1)),
                dma((CHUNKS, n_tm - 1)),
                dma((CHUNKS, n_tm - 1)),
            ],
            compiler_params=pltpu.CompilerParams(
                collective_id=0, has_side_effects=True, vmem_limit_bytes=32 << 20
            ),
        )(
            pltpu.with_memory_space_constraint(returns, pltpu.HBM),
            pltpu.with_memory_space_constraint(weights, pltpu.HBM),
        )

    in_specs = (P("tm", "paths", None), P("paths", None))
    out_specs = P("tm", "paths")
    return jax.shard_map(shards, mesh=mesh, in_specs=in_specs, out_specs=out_specs, check_vma=False)
```

time: 16.6 us -> 15.7 us (0.946)
  Pallas kernels: 15.9 us -> 14.9 us
    pallas_call x1, Pallas kernels: 15.9 us -> 14.9 us  [shards(): pl.pallas_call(functools.partial(kernel, n_tm, n_paths), out_shape=jax.Sh...]
where the time goes in v3:
time: 15.7 us; the launch traced here: 15.6 us
  Pallas kernels  14.9 us (95%)
  local copies, waits for them, and re-layouts  0.62 us (4%)
    pallas_call x1, Pallas kernels, shards(): pl.pallas_call(functools.partial(kernel, n_tm, n_paths), out_shape=jax.Sh...  14.9 us
    unnamed x1, local copies, waits for them, and re-layouts  0.62 us

profile of v3, /device:TPU:0, one launch (start us, length us, event | category | flops | bytes accessed | tf_op | source)
XLA Modules:
  0.0 15.6 jit_solution(18440961524361660042)
XLA Ops:
  0.0 14.9 %shard_map.28 = f32[16,512]{1,0:T(8,128)S(1)} custom-call(bf16[32,512,256]{2,1,0:T(8,128)(2,1)} %ret_hbm.1, bf16[32,64]{1,0:T(8,128)(2,1)} %w_hbm.1), custom_call_target="tpu_custom_call" | custom-call | tf_op jit(solution)/shard_map/pallas_call | solution.py:288
  15.0 0.6 %copy.4 = f32[16,512]{1,0:T(8,128)} copy(f32[16,512]{1,0:T(8,128)S(1)} %shard_map.28) | data formatting | bytes 65536

commit v4 on v3

--- a/solution.py
+++ b/solution.py
@@ -10,7 +10,9 @@
 MESH = pl.DeviceIdType.MESH
 CHUNKS = 2
 ROWS = 32
-LOUD = 32
+PIECES = 8
+AHEAD = 8
+LOUD = 64
 END, FALL, DIP, LOSS = range(4)
 TOP = 2.0**15.75
 TINY = 1e-30
@@ -18,8 +20,8 @@
 
 def kernel(
     n_tm, n_paths, ret_hbm, w_hbm, out_ref,
-    ret, own_w, pair_w, wbuf, part, more, send, recv, loud, louds,
-    load_sem, own_sem, ready, near_sem, far_sem, wrecv_sem, send_sem, recv_sem, lsend_sem, lrecv_sem,
+    ret, own_w, pair_w, wbuf, part, more, send, recv, loud, louds, values,
+    load_sem, own_sem, ready, opened, near_sem, far_sem, wrecv_sem, send_sem, recv_sem, lsend_sem, lrecv_sem,
 ):
     steps, paths, assets = ret.shape
     ports = own_w.shape[1]
@@ -33,7 +35,8 @@
     share = own_w.shape[0]
 
     bits = [1 << i for i in range(n_tm.bit_length() - 1)]
-    others = range(n_tm - 1, 0, -1)
+    others = sorted(range(1, n_tm), key=lambda k: -k.bit_count())
+    arrivals = others[::-1]
 
     def across(k):
         other = tm
@@ -59,7 +62,7 @@
     pl.when(upper == 1)(lambda: greet(tm, gate))
     pl.when(upper == 0)(greet_upper)
     for k in range(1, half_axis):
-        greet(tm, fellow(k))
+        pl.when(fellow(k) != gate)(lambda: greet(tm, fellow(k)))
     for k in bits:
         greet(across(k), me)
 
@@ -67,20 +70,22 @@
     own.start()
 
     def load(c):
-        rows = pl.ds(c * width, width)
-        return pltpu.make_async_copy(ret_hbm.at[:, rows], ret.at[:, rows], load_sem.at[c])
-
-    for c in range(CHUNKS):
+        days = pl.ds(c * (steps // PIECES), steps // PIECES)
+        return pltpu.make_async_copy(ret_hbm.at[days], ret.at[days], load_sem.at[c])
+
+    for c in range(AHEAD):
         load(c).start(priority=1)
 
     own.wait()
     pair_w[...] = jnp.concatenate([own_w[0 : share // 2], own_w[share // 2 :]], axis=1)
     wbuf[me] = pair_w[...]
-    crossing = jnp.logical_or(upper == 1, me == gate).astype(jnp.int32)
-    pl.semaphore_wait(barrier, half_axis - 1 + len(bits) + half_axis * crossing)
-
-    for k in (k for k in range(n_tm) if k.bit_count() == 2):
-        pl.semaphore_signal(ready.at[k], inc=1, device_id=(across(k & -k), me), device_id_type=MESH)
+    pl.when(me != gate)(lambda: pl.semaphore_wait(barrier, half_axis - 1 + len(bits) + half_axis * upper))
+
+    def open_gate():
+        pl.semaphore_signal(opened, inc=1, device_id=(tm, gate), device_id_type=MESH)
+
+    pl.when(jnp.logical_and(upper == 0, me != gate))(open_gate)
+    pl.when(me == gate)(lambda: pl.semaphore_wait(opened, half_axis - 1))
 
     def block_of_weights(slot, count, target, sem):
         rows = pl.ds(slot, count)
@@ -134,8 +139,16 @@
 
     send_down(lambda copy: copy.start())
     send_near(lambda copy: copy.start())
-    for k in range(1, half_axis):
-        arrival(fellow(k), 1)
+    pl.when(me == gate)(lambda: pl.semaphore_wait(barrier, half_axis + len(bits)))
+
+    for k in (k for k in range(n_tm) if k.bit_count() == 2):
+        pl.semaphore_signal(ready.at[k], inc=1, device_id=(across(k & -k), me), device_id_type=MESH)
+
+    def near_arrival():
+        for k in range(1, half_axis):
+            arrival(fellow(k), 1)
+
+    pl.when(me == gate)(near_arrival)
     send_over(lambda copy: copy.start())
 
     for p in range(2, len(bits) + 1):
@@ -144,15 +157,34 @@
         for k in (k for k in range(n_tm) if k.bit_count() == p + 1):
             pl.semaphore_signal(ready.at[k], inc=1, device_id=(across(k & -k), me), device_id_type=MESH)
 
-    def loud_copy(c, k, slot):
+    def loud_copy(k, slot):
         return pltpu.make_async_remote_copy(
-            src_ref=loud.at[c],
-            dst_ref=louds.at[c, slot],
-            send_sem=lsend_sem.at[c, k - 1],
-            recv_sem=lrecv_sem.at[c, k - 1],
+            src_ref=loud,
+            dst_ref=louds.at[slot],
+            send_sem=lsend_sem.at[k - 1],
+            recv_sem=lrecv_sem.at[k - 1],
             device_id=(across(k), me),
             device_id_type=MESH,
         )
+
+    top = jnp.zeros((LOUD, assets), ret.dtype)
+    for c in range(PIECES):
+        load(c).wait()
+        if c + AHEAD < PIECES:
+            load(c + AHEAD).start(priority=1)
+
+        def look(i, top):
+            t, r = c * (steps // PIECES) + i // (paths // (4 * LOUD)), i % (paths // (4 * LOUD)) * (4 * LOUD)
+            for q in range(4):
+                top = jnp.maximum(top, jnp.abs(ret[t, pl.ds(r + q * LOUD, LOUD)]))
+            return top
+
+        top = lax.fori_loop(0, steps // PIECES * (paths // (4 * LOUD)), look, top)
+    loud[...] = jnp.full(loud.shape, jnp.max(top.astype(jnp.float32)), jnp.float32)
+    for k in others:
+        loud_copy(k, tm).start()
+    louds[tm] = loud[...]
+    pl.when(me != gate)(near_arrival)
 
     def side(h):
         held = wbuf[pl.ds(h * half_axis, half_axis)]
@@ -187,10 +219,13 @@
         pl.when(s == n_tm - 1)(lambda: act(FALL, 2))
         pl.when(jnp.logical_and(s > 0, s < n_tm - 1))(lambda: act(END, 4))
 
-    def send_blocks(c, act):
+    def send_blocks(c, act, late):
         def blocks(first, count):
             for k in others:
-                act(block_copy(c, k, tm, first, count))
+                if k.bit_count() > 1:
+                    pl.when((across(k) > 0) == late)(lambda: act(block_copy(c, k, tm, first, count)))
+                elif not late:
+                    act(block_copy(c, k, tm, first, count))
 
         by_segment(tm, blocks)
 
@@ -200,17 +235,8 @@
 
     both = side(upper)
     for c in range(CHUNKS):
-        load(c).wait()
         for i in range(subs):
             part[c, i] = product(c, i, upper, both)
-        top = jnp.zeros((LOUD, assets), ret.dtype)
-        for t in range(steps):
-            for r in range(c * width, (c + 1) * width, LOUD):
-                top = jnp.maximum(top, jnp.abs(ret[t, r : r + LOUD]))
-        loud[c] = jnp.full(loud.shape[1:], jnp.max(top.astype(jnp.float32)), jnp.float32)
-        for k in others:
-            loud_copy(c, k, tm).start()
-        louds[c, tm] = loud[c]
 
     far_arrival()
     both = side(1 - upper)
@@ -219,7 +245,7 @@
             more[c, i] = product(c, i, 1 - upper, both)
         if c == 0:
             heavy = jnp.max(jnp.abs(wbuf[...].astype(jnp.float32))) * (assets * steps)
-        scale = TOP / jnp.maximum(loud[c, 0:1] * heavy, TINY)
+        scale = TOP / jnp.maximum(loud[0:1] * heavy, TINY)
         pieces = []
         for i in range(subs):
             zero = jnp.zeros((ROWS, 2 * ports), jnp.float32)
@@ -246,34 +272,39 @@
                 rows = b * block
                 send[c, b, k, :, 0:half] = whole[rows : rows + block]
                 send[c, b, k, :, half:width] = whole[ports + rows : ports + rows + block]
-        send_blocks(c, lambda copy: copy.start())
-        recv[c, tm] = send[c, tm]
-
-    def figure(c, s, k, back):
-        code = recv[c, s, k].astype(jnp.float32)
-        size = jnp.exp(jnp.log(jnp.abs(code)) * 0.125) * back[s]
-        return jnp.where(code < 0, -size, size) if k == LOSS else size
-
-    for c in range(CHUNKS):
-        for k in others:
-            block_arrival(c, k)
-            loud_copy(c, k, across(k)).wait_recv()
-        back = jnp.maximum(louds[c, :, 0:1] * heavy, TINY) / TOP
-        back = jnp.concatenate([back] * (width // back.shape[2]), axis=2)
-        end, fall = figure(c, 0, END, back), figure(c, 0, FALL, back)
-        for s in range(1, n_tm):
-            fall = jnp.maximum(jnp.maximum(fall, figure(c, s, FALL, back)), end + figure(c, s, DIP, back))
-            if s < n_tm - 1:
-                end = jnp.maximum(end + figure(c, s, LOSS, back), figure(c, s, END, back))
-        out_ref[:, pl.ds(c * width, width)] = fall
-
+        send_blocks(c, lambda copy: copy.start(), False)
+
+    for c in range(CHUNKS):
+        send_blocks(c, lambda copy: copy.start(), True)
     send_down(lambda copy: copy.wait_send())
     send_near(lambda copy: copy.wait_send())
     send_over(lambda copy: copy.wait_send())
-    for c in range(CHUNKS):
-        for k in others:
-            loud_copy(c, k, tm).wait_send()
-        send_blocks(c, lambda copy: copy.wait_send())
+    for k in others:
+        loud_copy(k, tm).wait_send()
+        loud_copy(k, across(k)).wait_recv()
+
+    def decode(codes, s):
+        unit = jnp.maximum(louds[s, 0:1] * heavy, TINY) / TOP
+        unit = jnp.concatenate([unit] * (width // unit.shape[1]), axis=1)
+        code = codes.astype(jnp.float32)
+        size = jnp.exp(jnp.log(jnp.abs(code)) * 0.125) * unit[None]
+        values[s] = jnp.concatenate([size[:LOSS], jnp.where(code[LOSS:] < 0, -size[LOSS:], size[LOSS:])], axis=0)
+
+    for c in range(CHUNKS):
+        decode(send[c, tm], tm)
+        for k in arrivals:
+            block_arrival(c, k)
+            decode(recv[c, across(k)], across(k))
+        end, fall = values[0, END], values[0, FALL]
+        for s in range(1, n_tm):
+            fall = jnp.maximum(jnp.maximum(fall, values[s, FALL]), end + values[s, DIP])
+            if s < n_tm - 1:
+                end = jnp.maximum(end + values[s, LOSS], values[s, END])
+        out_ref[:, pl.ds(c * width, width)] = fall
+
+    for c in range(CHUNKS):
+        for late in (False, True):
+            send_blocks(c, lambda copy: copy.wait_send(), late)
 
 
 def solution(mesh):
@@ -302,18 +333,20 @@
                 pltpu.VMEM((CHUNKS, subs, steps, ROWS, 2 * ports), jnp.float32),
                 pltpu.VMEM((CHUNKS, n_tm, 4, block, width), jnp.bfloat16),
                 pltpu.VMEM((CHUNKS, n_tm, 4, block, width), jnp.bfloat16),
-                pltpu.VMEM((CHUNKS, 8, 2 * ports), jnp.float32),
-                pltpu.VMEM((CHUNKS, n_tm, 8, 2 * ports), jnp.float32),
-                dma((CHUNKS,)),
+                pltpu.VMEM((8, 2 * ports), jnp.float32),
+                pltpu.VMEM((n_tm, 8, 2 * ports), jnp.float32),
+                pltpu.VMEM((n_tm, 4, block, width), jnp.float32),
+                dma((PIECES,)),
                 dma,
                 pltpu.SemaphoreType.REGULAR((n_tm,)),
+                pltpu.SemaphoreType.REGULAR,
                 dma((n_paths // 2 - 1,)),
                 dma((n_paths // 2,)),
                 dma((n_paths,)),
                 dma((CHUNKS, n_tm - 1)),
                 dma((CHUNKS, n_tm - 1)),
-                dma((CHUNKS, n_tm - 1)),
-                dma((CHUNKS, n_tm - 1)),
+                dma((n_tm - 1,)),
+                dma((n_tm - 1,)),
             ],
             compiler_params=pltpu.CompilerParams(
                 collective_id=0, has_side_effects=True, vmem_limit_bytes=32 << 20

time: 15.7 us -> 15 us (0.955)
  Pallas kernels: 14.9 us -> 14.3 us
    pallas_call x1, Pallas kernels: 14.9 us -> 14.3 us  [shards(): pl.pallas_call(functools.partial(kernel, n_tm, n_paths), out_shape=jax.Sh...]
where the time goes in v4:
time: 15 us; the launch traced here: 14.9 us
  Pallas kernels  14.3 us (95%)
  local copies, waits for them, and re-layouts  0.62 us (4%)
    pallas_call x1, Pallas kernels, shards(): pl.pallas_call(functools.partial(kernel, n_tm, n_paths), out_shape=jax.Sh...  14.3 us
    unnamed x1, local copies, waits for them, and re-layouts  0.62 us

profile of v4, /device:TPU:0, one launch (start us, length us, event | category | flops | bytes accessed | tf_op | source)
XLA Modules:
  0.0 14.9 jit_solution(1386478626941931442)
XLA Ops:
  0.0 14.3 %shard_map.28 = f32[16,512]{1,0:T(8,128)S(1)} custom-call(bf16[32,512,256]{2,1,0:T(8,128)(2,1)} %ret_hbm.1, bf16[32,64]{1,0:T(8,128)(2,1)} %w_hbm.1), custom_call_target="tpu_custom_call" | custom-call | tf_op jit(solution)/shard_map/pallas_call | solution.py:319
  14.3 0.6 %copy.4 = f32[16,512]{1,0:T(8,128)} copy(f32[16,512]{1,0:T(8,128)S(1)} %shard_map.28) | data formatting | bytes 65536

commit v5 on v4

--- a/solution.py
+++ b/solution.py
@@ -10,8 +10,7 @@
 MESH = pl.DeviceIdType.MESH
 CHUNKS = 2
 ROWS = 32
-PIECES = 8
-AHEAD = 8
+PIECES = 4
 LOUD = 64
 END, FALL, DIP, LOSS = range(4)
 TOP = 2.0**15.75
@@ -21,7 +20,7 @@
 def kernel(
     n_tm, n_paths, ret_hbm, w_hbm, out_ref,
     ret, own_w, pair_w, wbuf, part, more, send, recv, loud, louds, values,
-    load_sem, own_sem, ready, opened, near_sem, far_sem, wrecv_sem, send_sem, recv_sem, lsend_sem, lrecv_sem,
+    load_sem, own_sem, ready, opened, near_sem, near_recv_sem, far_sem, far_recv_sem, send_sem, recv_sem, lsend_sem, lrecv_sem,
 ):
     steps, paths, assets = ret.shape
     ports = own_w.shape[1]
@@ -34,9 +33,12 @@
     me = lax.axis_index("paths")
     share = own_w.shape[0]
 
+    own = pltpu.make_async_copy(w_hbm, own_w, own_sem)
+    own.start()
     bits = [1 << i for i in range(n_tm.bit_length() - 1)]
     others = sorted(range(1, n_tm), key=lambda k: -k.bit_count())
     arrivals = others[::-1]
+    apart = [k for k in others if k.bit_count() > 1]
 
     def across(k):
         other = tm
@@ -66,14 +68,12 @@
     for k in bits:
         greet(across(k), me)
 
-    own = pltpu.make_async_copy(w_hbm, own_w, own_sem)
-    own.start()
 
     def load(c):
         days = pl.ds(c * (steps // PIECES), steps // PIECES)
         return pltpu.make_async_copy(ret_hbm.at[days], ret.at[days], load_sem.at[c])
 
-    for c in range(AHEAD):
+    for c in range(PIECES):
         load(c).start(priority=1)
 
     own.wait()
@@ -87,82 +87,70 @@
     pl.when(jnp.logical_and(upper == 0, me != gate))(open_gate)
     pl.when(me == gate)(lambda: pl.semaphore_wait(opened, half_axis - 1))
 
-    def block_of_weights(slot, count, target, sem):
-        rows = pl.ds(slot, count)
+    def weights_copy(source, rows, target, sems):
         return pltpu.make_async_remote_copy(
-            src_ref=wbuf.at[rows],
+            src_ref=source,
             dst_ref=wbuf.at[rows],
-            send_sem=sem,
-            recv_sem=wrecv_sem.at[slot],
+            send_sem=sems[0],
+            recv_sem=sems[1],
             device_id=(tm, target),
             device_id_type=MESH,
         )
 
-    def own_weights(target, sem):
-        return pltpu.make_async_remote_copy(
-            src_ref=pair_w,
-            dst_ref=wbuf.at[me],
-            send_sem=sem,
-            recv_sem=wrecv_sem.at[me],
-            device_id=(tm, target),
-            device_id_type=MESH,
-        )
-
-    def arrival(slot, count):
-        block_of_weights(slot, count, me, near_sem.at[0]).wait_recv()
+    def weights_wait(count, sems):
+        rows = pl.ds(0, count)
+        return weights_copy(wbuf.at[rows], rows, gate, sems)
+
+    near_sems = near_sem, near_recv_sem
+
+    def far_sems(p):
+        return far_sem.at[p], far_recv_sem
 
     def send_down(act):
         def down():
             for p in range(half_axis):
-                act(own_weights(p, far_sem.at[p]))
+                act(weights_copy(pair_w, me, p, far_sems(p)))
 
         pl.when(upper == 1)(down)
 
     def send_near(act):
         for k in range(half_axis - 1, 0, -1):
-            act(own_weights(fellow(k), near_sem.at[k - 1]))
+            act(weights_copy(pair_w, me, fellow(k), near_sems))
 
     def send_over(act):
+        rows = pl.ds(0, half_axis)
+
         def over():
-            for p in range(n_paths - 1, half_axis - 1, -1):
-                act(block_of_weights(0, half_axis, p, far_sem.at[p - half_axis]))
+            for p in range(half_axis - 1, -1, -1):
+                act(weights_copy(wbuf.at[rows], rows, half_axis + p, far_sems(p)))
 
         pl.when(me == gate)(over)
-
-    def far_arrival():
-        def shards():
-            for p in range(half_axis, n_paths):
-                arrival(p, 1)
-
-        pl.when(upper == 1)(lambda: arrival(0, half_axis))
-        pl.when(upper == 0)(shards)
 
     send_down(lambda copy: copy.start())
     send_near(lambda copy: copy.start())
     pl.when(me == gate)(lambda: pl.semaphore_wait(barrier, half_axis + len(bits)))
 
     for k in (k for k in range(n_tm) if k.bit_count() == 2):
-        pl.semaphore_signal(ready.at[k], inc=1, device_id=(across(k & -k), me), device_id_type=MESH)
+        pl.semaphore_signal(ready.at[apart.index(k)], inc=1, device_id=(across(k & -k), me), device_id_type=MESH)
 
     def near_arrival():
-        for k in range(1, half_axis):
-            arrival(fellow(k), 1)
+        weights_wait(half_axis - 1, near_sems).wait_recv()
 
     pl.when(me == gate)(near_arrival)
     send_over(lambda copy: copy.start())
 
     for p in range(2, len(bits) + 1):
         for k in (k for k in range(n_tm) if k.bit_count() == p):
-            pl.semaphore_wait(ready.at[k], 1)
+            pl.semaphore_wait(ready.at[apart.index(k)], 1)
         for k in (k for k in range(n_tm) if k.bit_count() == p + 1):
-            pl.semaphore_signal(ready.at[k], inc=1, device_id=(across(k & -k), me), device_id_type=MESH)
-
-    def loud_copy(k, slot):
+            pl.semaphore_signal(ready.at[apart.index(k)], inc=1, device_id=(across(k & -k), me), device_id_type=MESH)
+
+    def loud_copy(k, source, slot):
         return pltpu.make_async_remote_copy(
-            src_ref=loud,
+            src_ref=source,
             dst_ref=louds.at[slot],
-            send_sem=lsend_sem.at[k - 1],
-            recv_sem=lrecv_sem.at[k - 1],
+            send_sem=lsend_sem,
+            recv_sem=lrecv_sem,
             device_id=(across(k), me),
             device_id_type=MESH,
         )
@@ -170,8 +158,6 @@
     top = jnp.zeros((LOUD, assets), ret.dtype)
     for c in range(PIECES):
         load(c).wait()
-        if c + AHEAD < PIECES:
-            load(c + AHEAD).start(priority=1)
 
         def look(i, top):
             t, r = c * (steps // PIECES) + i // (paths // (4 * LOUD)), i % (paths // (4 * LOUD)) * (4 * LOUD)
@@ -182,7 +168,7 @@
         top = lax.fori_loop(0, steps // PIECES * (paths // (4 * LOUD)), look, top)
     loud[...] = jnp.full(loud.shape, jnp.max(top.astype(jnp.float32)), jnp.float32)
     for k in others:
-        loud_copy(k, tm).start()
+        loud_copy(k, loud, tm).start()
     louds[tm] = loud[...]
     pl.when(me != gate)(near_arrival)
 
@@ -203,13 +189,13 @@
             jnp.concatenate([first, second], axis=1), both, preferred_element_type=jnp.float32
         ).reshape(steps, ROWS, 2 * ports)
 
-    def block_copy(c, k, slot, first, count):
+    def block_copy(c, k, target, slot, first, count):
         figures = pl.ds(first, count)
         return pltpu.make_async_remote_copy(
-            src_ref=send.at[c, across(k), figures],
+            src_ref=send.at[c, target, figures],
             dst_ref=recv.at[c, slot, figures],
-            send_sem=send_sem.at[c, k - 1],
-            recv_sem=recv_sem.at[c, k - 1],
+            send_sem=send_sem,
+            recv_sem=recv_sem.at[c, k - 1] if isinstance(c, int) else recv_sem.at[0, 0],
             device_id=(across(k), me),
             device_id_type=MESH,
         )
@@ -223,22 +209,22 @@
         def blocks(first, count):
             for k in others:
                 if k.bit_count() > 1:
-                    pl.when((across(k) > 0) == late)(lambda: act(block_copy(c, k, tm, first, count)))
+                    pl.when((across(k) > 0) == late)(lambda: act(block_copy(c, k, across(k), tm, first, count)))
                 elif not late:
-                    act(block_copy(c, k, tm, first, count))
+                    act(block_copy(c, k, across(k), tm, first, count))
 
         by_segment(tm, blocks)
 
     def block_arrival(c, k):
         s = across(k)
-        by_segment(s, lambda first, count: block_copy(c, k, s, first, count).wait_recv())
+        by_segment(s, lambda first, count: block_copy(c, k, s, s, first, count).wait_recv())
 
     both = side(upper)
     for c in range(CHUNKS):
         for i in range(subs):
             part[c, i] = product(c, i, upper, both)
 
-    far_arrival()
+    weights_wait(half_axis, far_sems(0)).wait_recv()
     both = side(1 - upper)
     for c in range(CHUNKS):
         for i in range(subs):
@@ -277,11 +263,11 @@
     for c in range(CHUNKS):
         send_blocks(c, lambda copy: copy.start(), True)
     send_down(lambda copy: copy.wait_send())
-    send_near(lambda copy: copy.wait_send())
+    weights_wait(half_axis - 1, near_sems).wait_send()
     send_over(lambda copy: copy.wait_send())
-    for k in others:
-        loud_copy(k, tm).wait_send()
-        loud_copy(k, across(k)).wait_recv()
+    rest = pl.ds(0, n_tm - 1)
+    loud_copy(1, louds.at[rest], rest).wait_send()
+    loud_copy(1, louds.at[rest], rest).wait_recv()
 
     def decode(codes, s):
         unit = jnp.maximum(louds[s, 0:1] * heavy, TINY) / TOP
@@ -290,9 +276,14 @@
         size = jnp.exp(jnp.log(jnp.abs(code)) * 0.125) * unit[None]
         values[s] = jnp.concatenate([size[:LOSS], jnp.where(code[LOSS:] < 0, -size[LOSS:], size[LOSS:])], axis=0)
 
+    def drain(first, count):
+        block_copy(pl.ds(0, CHUNKS), 1, rest, rest, first, count).wait_send()
+
     for c in range(CHUNKS):
         decode(send[c, tm], tm)
         for k in arrivals:
+            if (c, k) == (CHUNKS - 1, arrivals[-1]):
+                by_segment(tm, drain)
             block_arrival(c, k)
             decode(recv[c, across(k)], across(k))
         end, fall = values[0, END], values[0, FALL]
@@ -301,10 +292,6 @@
             if s < n_tm - 1:
                 end = jnp.maximum(end + values[s, LOSS], values[s, END])
         out_ref[:, pl.ds(c * width, width)] = fall
-
-    for c in range(CHUNKS):
-        for late in (False, True):
-            send_blocks(c, lambda copy: copy.wait_send(), late)
 
 
 def solution(mesh):
@@ -338,15 +325,16 @@
                 pltpu.VMEM((n_tm, 4, block, width), jnp.float32),
                 dma((PIECES,)),
                 dma,
-                pltpu.SemaphoreType.REGULAR((n_tm,)),
+                pltpu.SemaphoreType.REGULAR((n_tm - n_tm.bit_length(),)),
                 pltpu.SemaphoreType.REGULAR,
-                dma((n_paths // 2 - 1,)),
+                dma,
+                dma,
                 dma((n_paths // 2,)),
-                dma((n_paths,)),
+                dma,
+                dma,
                 dma((CHUNKS, n_tm - 1)),
-                dma((CHUNKS, n_tm - 1)),
-                dma((n_tm - 1,)),
-                dma((n_tm - 1,)),
+                dma,
+                dma,
             ],
             compiler_params=pltpu.CompilerParams(
                 collective_id=0, has_side_effects=True, vmem_limit_bytes=32 << 20

time: 15 us -> 14.9 us (level)
  Pallas kernels: 14.3 us -> 14 us
    pallas_call x1, Pallas kernels: 14.3 us -> 14 us  [shards(): pl.pallas_call(functools.partial(kernel, n_tm, n_paths), out_shape=jax.Sh...]
where the time goes in v5:
time: 14.9 us; the launch traced here: 14.7 us
  Pallas kernels  14 us (94%)
  local copies, waits for them, and re-layouts  0.62 us (4%)
    pallas_call x1, Pallas kernels, shards(): pl.pallas_call(functools.partial(kernel, n_tm, n_paths), out_shape=jax.Sh...  14 us
    unnamed x1, local copies, waits for them, and re-layouts  0.62 us

profile of v5, /device:TPU:0, one launch (start us, length us, event | category | flops | bytes accessed | tf_op | source)
XLA Modules:
  0.0 14.7 jit_solution(1655944486793221463)
XLA Ops:
  0.0 14.0 %shard_map.28 = f32[16,512]{1,0:T(8,128)S(1)} custom-call(bf16[32,512,256]{2,1,0:T(8,128)(2,1)} %ret_hbm.1, bf16[32,64]{1,0:T(8,128)(2,1)} %w_hbm.1), custom_call_target="tpu_custom_call" | custom-call | tf_op jit(solution)/shard_map/pallas_call | solution.py:306
  14.0 0.6 %copy.4 = f32[16,512]{1,0:T(8,128)} copy(f32[16,512]{1,0:T(8,128)S(1)} %shard_map.28) | data formatting | bytes 65536

commit v6 on v5

--- a/solution.py
+++ b/solution.py
@@ -20,7 +20,7 @@
 def kernel(
     n_tm, n_paths, ret_hbm, w_hbm, out_ref,
     ret, own_w, pair_w, wbuf, part, more, send, recv, loud, louds, values,
-    load_sem, own_sem, ready, opened, near_sem, near_recv_sem, far_sem, far_recv_sem, send_sem, recv_sem, lsend_sem, lrecv_sem,
+    load_sem, own_sem, told, opened, near_sem, near_recv_sem, far_sem, far_recv_sem, send_sem, recv_sem, lsend_sem, lrecv_sem,
 ):
     steps, paths, assets = ret.shape
     ports = own_w.shape[1]
@@ -38,7 +38,6 @@
     bits = [1 << i for i in range(n_tm.bit_length() - 1)]
     others = sorted(range(1, n_tm), key=lambda k: -k.bit_count())
     arrivals = others[::-1]
-    apart = [k for k in others if k.bit_count() > 1]
 
     def across(k):
         other = tm
@@ -65,8 +64,12 @@
     pl.when(upper == 0)(greet_upper)
     for k in range(1, half_axis):
         pl.when(fellow(k) != gate)(lambda: greet(tm, fellow(k)))
-    for k in bits:
-        greet(across(k), me)
+
+    def greet_across():
+        for k in bits:
+            greet(across(k), me)
+
+    pl.when(upper == 0)(greet_across)
 
 
     def load(c):
@@ -79,7 +82,7 @@
     own.wait()
     pair_w[...] = jnp.concatenate([own_w[0 : share // 2], own_w[share // 2 :]], axis=1)
     wbuf[me] = pair_w[...]
-    pl.when(me != gate)(lambda: pl.semaphore_wait(barrier, half_axis - 1 + len(bits) + half_axis * upper))
+    pl.when(me != gate)(lambda: pl.semaphore_wait(barrier, half_axis - 1 + len(bits) * (1 - upper) + half_axis * upper))
 
     def open_gate():
         pl.semaphore_signal(opened, inc=1, device_id=(tm, gate), device_id_type=MESH)
@@ -130,20 +133,22 @@
     send_near(lambda copy: copy.start())
     pl.when(me == gate)(lambda: pl.semaphore_wait(barrier, half_axis + len(bits)))
 
-    for k in (k for k in range(n_tm) if k.bit_count() == 2):
-        pl.semaphore_signal(ready.at[apart.index(k)], inc=1, device_id=(across(k & -k), me), device_id_type=MESH)
+    def tell(p):
+        for k in (k for k in others if k.bit_count() == p):
+            pl.semaphore_signal(told.at[k - 1], inc=1, device_id=(across(k & -k), me), device_id_type=MESH)
+
+    def hear(p):
+        for k in (k for k in others if k.bit_count() == p):
+            pl.semaphore_wait(told.at[k - 1], 1)
+
+    pl.when(me == gate)(lambda: tell(1))
+    pl.when(me < gate)(lambda: tell(2))
 
     def near_arrival():
         weights_wait(half_axis - 1, near_sems).wait_recv()
 
     pl.when(me == gate)(near_arrival)
     send_over(lambda copy: copy.start())
-
-    for p in range(2, len(bits) + 1):
-        for k in (k for k in range(n_tm) if k.bit_count() == p):
-            pl.semaphore_wait(ready.at[apart.index(k)], 1)
-        for k in (k for k in range(n_tm) if k.bit_count() == p + 1):
-            pl.semaphore_signal(ready.at[apart.index(k)], inc=1, device_id=(across(k & -k), me), device_id_type=MESH)
 
     def loud_copy(k, source, slot):
         return pltpu.make_async_remote_copy(
@@ -167,10 +172,14 @@
 
         top = lax.fori_loop(0, steps // PIECES * (paths // (4 * LOUD)), look, top)
     loud[...] = jnp.full(loud.shape, jnp.max(top.astype(jnp.float32)), jnp.float32)
-    for k in others:
-        loud_copy(k, loud, tm).start()
     louds[tm] = loud[...]
     pl.when(me != gate)(near_arrival)
+
+    def gates():
+        hear(1)
+        tell(2)
+
+    pl.when(me == gate)(gates)
 
     def side(h):
         held = wbuf[pl.ds(h * half_axis, half_axis)]
@@ -223,6 +232,21 @@
     for c in range(CHUNKS):
         for i in range(subs):
             part[c, i] = product(c, i, upper, both)
+
+    def spread():
+        for p in range(2, len(bits) + 1):
+            hear(p)
+            tell(p + 1)
+
+    def admit():
+        for p in range(half_axis, n_paths):
+            pl.semaphore_signal(told.at[0], inc=1, device_id=(tm, p), device_id_type=MESH)
+
+    pl.when(upper == 0)(spread)
+    pl.when(me == gate)(admit)
+    pl.when(upper == 1)(lambda: pl.semaphore_wait(told.at[0], 1))
+    for k in others:
+        loud_copy(k, loud, tm).start()
 
     weights_wait(half_axis, far_sems(0)).wait_recv()
     both = side(1 - upper)
@@ -325,7 +349,7 @@
                 pltpu.VMEM((n_tm, 4, block, width), jnp.float32),
                 dma((PIECES,)),
                 dma,
-                pltpu.SemaphoreType.REGULAR((n_tm - n_tm.bit_length(),)),
+                pltpu.SemaphoreType.REGULAR((n_tm - 1,)),
                 pltpu.SemaphoreType.REGULAR,
                 dma,
                 dma,

time: 14.9 us -> 14.5 us (0.973)
  Pallas kernels: 14 us -> 13.7 us
    pallas_call x1, Pallas kernels: 14 us -> 13.7 us  [shards(): pl.pallas_call(functools.partial(kernel, n_tm, n_paths), out_shape=jax.Sh...]
where the time goes in v6:
time: 14.5 us; the launch traced here: 14.3 us
  Pallas kernels  13.7 us (94%)
  local copies, waits for them, and re-layouts  0.62 us (4%)
    pallas_call x1, Pallas kernels, shards(): pl.pallas_call(functools.partial(kernel, n_tm, n_paths), out_shape=jax.Sh...  13.7 us
    unnamed x1, local copies, waits for them, and re-layouts  0.62 us

profile of v6, /device:TPU:0, one launch (start us, length us, event | category | flops | bytes accessed | tf_op | source)
XLA Modules:
  0.0 14.3 jit_solution(5635761975905012597)
XLA Ops:
  0.0 13.7 %shard_map.28 = f32[16,512]{1,0:T(8,128)S(1)} custom-call(bf16[32,512,256]{2,1,0:T(8,128)(2,1)} %ret_hbm.1, bf16[32,64]{1,0:T(8,128)(2,1)} %w_hbm.1), custom_call_target="tpu_custom_call" | custom-call | tf_op jit(solution)/shard_map/pallas_call | solution.py:330
  13.7 0.6 %copy.4 = f32[16,512]{1,0:T(8,128)} copy(f32[16,512]{1,0:T(8,128)S(1)} %shard_map.28) | data formatting | bytes 65536

commit v7 on v6

--- a/solution.py
+++ b/solution.py
@@ -19,7 +19,7 @@
 
 def kernel(
     n_tm, n_paths, ret_hbm, w_hbm, out_ref,
-    ret, own_w, pair_w, wbuf, part, more, send, recv, loud, louds, values,
+    ret, own_w, pair_w, wbuf, wraw, part, more, send, recv, loud, louds, values,
     load_sem, own_sem, told, opened, near_sem, near_recv_sem, far_sem, far_recv_sem, send_sem, recv_sem, lsend_sem, lrecv_sem,
 ):
     steps, paths, assets = ret.shape
@@ -79,9 +79,6 @@
     for c in range(PIECES):
         load(c).start(priority=1)
 
-    own.wait()
-    pair_w[...] = jnp.concatenate([own_w[0 : share // 2], own_w[share // 2 :]], axis=1)
-    wbuf[me] = pair_w[...]
     pl.when(me != gate)(lambda: pl.semaphore_wait(barrier, half_axis - 1 + len(bits) * (1 - upper) + half_axis * upper))
 
     def open_gate():
@@ -90,6 +87,7 @@
     pl.when(jnp.logical_and(upper == 0, me != gate))(open_gate)
     pl.when(me == gate)(lambda: pl.semaphore_wait(opened, half_axis - 1))
 
+    own.wait()
     def weights_copy(source, rows, target, sems):
         return pltpu.make_async_remote_copy(
             src_ref=source,
@@ -109,10 +107,20 @@
     def far_sems(p):
         return far_sem.at[p], far_recv_sem
 
+    def raw_copy(source, rows, p):
+        return pltpu.make_async_remote_copy(
+            src_ref=source,
+            dst_ref=wraw.at[rows],
+            send_sem=far_sem.at[p],
+            recv_sem=far_recv_sem,
+            device_id=(tm, p),
+            device_id_type=MESH,
+        )
+
     def send_down(act):
         def down():
             for p in range(half_axis):
-                act(weights_copy(pair_w, me, p, far_sems(p)))
+                act(raw_copy(own_w, me - half_axis, p))
 
         pl.when(upper == 1)(down)
 
@@ -130,6 +138,8 @@
         pl.when(me == gate)(over)
 
     send_down(lambda copy: copy.start())
+    pair_w[...] = jnp.concatenate([own_w[0 : share // 2], own_w[share // 2 :]], axis=1)
+    wbuf[me] = pair_w[...]
     send_near(lambda copy: copy.start())
     pl.when(me == gate)(lambda: pl.semaphore_wait(barrier, half_axis + len(bits)))
 
@@ -248,13 +258,21 @@
     for k in others:
         loud_copy(k, loud, tm).start()
 
-    weights_wait(half_axis, far_sems(0)).wait_recv()
-    both = side(1 - upper)
+    rows = pl.ds(0, half_axis)
+    pl.when(upper == 1)(lambda: weights_wait(half_axis, far_sems(0)).wait_recv())
+    pl.when(upper == 0)(lambda: raw_copy(wraw.at[rows], rows, 0).wait_recv())
+    raw = wraw[...].reshape(depth, ports)
+    blank = jnp.zeros_like(raw)
+    low = jnp.concatenate(
+        [jnp.concatenate([raw, blank], axis=1), jnp.concatenate([blank, raw], axis=1)], axis=0
+    )
+    near_top = jnp.max(jnp.abs(both.astype(jnp.float32)))
+    both = jnp.where(upper == 1, side(0), low)
     for c in range(CHUNKS):
         for i in range(subs):
             more[c, i] = product(c, i, 1 - upper, both)
         if c == 0:
-            heavy = jnp.max(jnp.abs(wbuf[...].astype(jnp.float32))) * (assets * steps)
+            heavy = jnp.maximum(near_top, jnp.max(jnp.abs(both.astype(jnp.float32)))) * (assets * steps)
         scale = TOP / jnp.maximum(loud[0:1] * heavy, TINY)
         pieces = []
         for i in range(subs):
@@ -340,6 +358,7 @@
                 pltpu.VMEM((share, ports), weights.dtype),
                 pltpu.VMEM((share // 2, 2 * ports), weights.dtype),
                 pltpu.VMEM((n_paths, share // 2, 2 * ports), weights.dtype),
+                pltpu.VMEM((n_paths // 2, share, ports), weights.dtype),
                 pltpu.VMEM((CHUNKS, subs, steps, ROWS, 2 * ports), jnp.float32),
                 pltpu.VMEM((CHUNKS, subs, steps, ROWS, 2 * ports), jnp.float32),
                 pltpu.VMEM((CHUNKS, n_tm, 4, block, width), jnp.bfloat16),

time: 14.5 us -> 14.5 us (level)
  no operation moved by 1% of the time
where the time goes in v7:
time: 14.5 us; the launch traced here: 14.4 us
  Pallas kernels  13.8 us (95%)
  local copies, waits for them, and re-layouts  0.62 us (4%)
    pallas_call x1, Pallas kernels, shards(): pl.pallas_call(functools.partial(kernel, n_tm, n_paths), out_shape=jax.Sh...  13.8 us
    unnamed x1, local copies, waits for them, and re-layouts  0.62 us

profile of v7, /device:TPU:0, one launch (start us, length us, event | category | flops | bytes accessed | tf_op | source)
XLA Modules:
  0.0 14.4 jit_solution(2974047129597632725)
XLA Ops:
  0.0 13.8 %shard_map.28 = f32[16,512]{1,0:T(8,128)S(1)} custom-call(bf16[32,512,256]{2,1,0:T(8,128)(2,1)} %ret_hbm.1, bf16[32,64]{1,0:T(8,128)(2,1)} %w_hbm.1), custom_call_target="tpu_custom_call" | custom-call | tf_op jit(solution)/shard_map/pallas_call | solution.py:348
  13.8 0.6 %copy.4 = f32[16,512]{1,0:T(8,128)} copy(f32[16,512]{1,0:T(8,128)S(1)} %shard_map.28) | data formatting | bytes 65536

commit v8 on v7

--- a/solution.py
+++ b/solution.py
@@ -9,7 +9,7 @@
 
 MESH = pl.DeviceIdType.MESH
 CHUNKS = 2
-ROWS = 32
+ROWS = 16
 PIECES = 4
 LOUD = 64
 END, FALL, DIP, LOSS = range(4)

time: 14.5 us -> 14.5 us (level)
  no operation moved by 1% of the time
where the time goes in v8:
time: 14.5 us; the launch traced here: 14.4 us
  Pallas kernels  13.7 us (94%)
  local copies, waits for them, and re-layouts  0.62 us (4%)
    pallas_call x1, Pallas kernels, shards(): pl.pallas_call(functools.partial(kernel, n_tm, n_paths), out_shape=jax.Sh...  13.7 us
    unnamed x1, local copies, waits for them, and re-layouts  0.62 us

profile of v8, /device:TPU:0, one launch (start us, length us, event | category | flops | bytes accessed | tf_op | source)
XLA Modules:
  0.0 14.4 jit_solution(4952296084948806523)
XLA Ops:
  0.0 13.7 %shard_map.28 = f32[16,512]{1,0:T(8,128)S(1)} custom-call(bf16[32,512,256]{2,1,0:T(8,128)(2,1)} %ret_hbm.1, bf16[32,64]{1,0:T(8,128)(2,1)} %w_hbm.1), custom_call_target="tpu_custom_call" | custom-call | tf_op jit(solution)/shard_map/pallas_call | solution.py:348
  13.8 0.6 %copy.4 = f32[16,512]{1,0:T(8,128)} copy(f32[16,512]{1,0:T(8,128)S(1)} %shard_map.28) | data formatting | bytes 65536
